TPU v7x, 256 devices: a whole 4x4x8 slice. The times are simulated.
256 devices in a mesh: dp: 8 (over z), vocab: 32 (over x, y, core).
Axes of the slice: x: 4, y: 4, z: 8, core: 2. Of those that a mesh axis runs over, the one named last changes fastest.
Arguments:
- hidden: bfloat16 [8, 2, 64, 4608], P('dp'), may hold values from -6 to 6
- table: bfloat16 [73728, 4608], P('vocab', 'dp'), may hold values from -0.25 to 0.25
- new_mask: int32 [73728], P('vocab'), may hold values from 0 to 1, as said below
- labels: int32 [8, 2, 64], P('dp'), may hold values from 0 to 73727
- in_grad: bfloat16 [8, 2, 768, 4608], P('dp', None, 'vocab'), may hold values from -0.75 to 0.75
- item_owner: int32 [8, 2, 768, 1], P('dp', None, 'vocab'), may hold values from 0 to 31; in each aligned block of 24 rows (0 to 23, 24 to 47, ..., all dimensions but the last counted through in order) at most 2 rows name the same one
- item_slot: int32 [8, 2, 768], P('dp', None, 'vocab'), may hold values from 0 to 255
- first_moment: float32 [8192, 4608], P('vocab', 'dp'), may hold values from -0.75 to 0.75
- second_moment: float32 [8192, 4608], P('vocab', 'dp'), may hold values from 0.0001 to 0.01
Outputs:
- token_loss: float32 [8, 2, 64], P('dp')
- d_hidden: bfloat16 [8, 2, 64, 4608], P('dp', None, None, 'vocab')
- update: float32 [8192, 4608], P('vocab', 'dp')
- first_out: float32 [8192, 4608], P('vocab', 'dp')
- second_out: float32 [8192, 4608], P('vocab', 'dp')
Inputs may be any that keep to these rules, and one draw needn't show every extreme that they name: `new_mask`: each aligned block of 2304 entries holds exactly 256 ones. `item_owner`: within the 24 rows of one device in one block, no shard is named more than 2 times, a bound that some block reaches.
All inputs are finite; a program needn't handle non-finite values.
Results may differ from a plain program's by a relative error of at most 0.006.
Values may be sent and summed in bfloat16 or wider, within the bound.
No kernel may reach another device: no remote copies, remote signals or barrier semaphores. Data moves between devices by JAX's collectives and lax.ppermute only.
A program may use at most 128 MiB of HBM per device.

v0:
```python
import jax
import jax.numpy as jnp
from jax import lax
from jax.sharding import PartitionSpec as P

cap_value = 30.0
beta_one = 0.9
beta_two = 0.95
step_count = 10
epsilon = 1e-08
decay_rate = 0.1


def sent_to_all(array, axis):
    peers = lax.axis_size(axis)
    return lax.all_to_all(
        jnp.broadcast_to(array[None], (peers, *array.shape)), axis, 0, 0, tiled=True
    )


def over_copies(array, axis):
    return sent_to_all(array, axis).sum(axis=0)


def packed_total(arrays, axis):
    line, at, gathered = (jnp.concatenate([a.reshape(-1) for a in arrays]), 0, [])
    subtotal = over_copies(line, axis)
    for a in arrays:
        gathered.append(subtotal[at : at + a.size].reshape(a.shape))
        at += a.size
    return tuple(gathered)


def in_blocks(array, dim, peers):
    shape = array.shape
    parts = array.reshape(*shape[:dim], peers, shape[dim] // peers, *shape[dim + 1 :])
    return jnp.moveaxis(parts, dim, 0)


def sent_and_summed(array, axis, dim):
    parts = in_blocks(array, dim, lax.axis_size(axis))
    arrived = lax.all_to_all(parts, axis, split_axis=0, concat_axis=0, tiled=True)
    return arrived.sum(axis=0)


def select_rows(new_mask, new_count):
    ranked = jnp.cumsum(new_mask) - 1
    wanted = (ranked[None, :] == jnp.arange(new_count, dtype=jnp.int32)[:, None]) & (
        new_mask[None, :] == 1
    )
    return wanted.astype(jnp.bfloat16)


def softmax_error(raw, label_row, vocab_start):
    capped = cap_value * jnp.tanh(raw / cap_value)
    expd = jnp.exp(capped)
    hits = jnp.arange(raw.shape[1], dtype=jnp.int32)[None, :] + vocab_start == label_row[:, None]
    local_total = jnp.sum(expd, axis=1)
    local_pick = jnp.sum(jnp.where(hits, capped, 0.0), axis=1)
    total, picked = packed_total((local_total, local_pick), "vocab")
    loss = jnp.log(total) - picked
    error = (
        (expd / total[:, None] - hits.astype(jnp.float32)) * (1.0 - (capped / cap_value) ** 2)
    ).astype(jnp.bfloat16)
    return (loss, error)


def finish_hidden(partial_value):
    return sent_and_summed(partial_value, "vocab", 1).astype(jnp.bfloat16)


def pack_items(rows, owner, slot, shards, capacity):
    onehot = (owner[:, None] == jnp.arange(shards, dtype=jnp.int32)[None, :]).astype(jnp.int32)
    running = jnp.cumsum(onehot, axis=0)
    ranked = jnp.sum(onehot * running, axis=1) - 1
    place = owner * capacity + ranked
    placing = jnp.arange(shards * capacity, dtype=jnp.int32)[:, None] == place[None, :]
    sent = jnp.dot(placing.astype(jnp.bfloat16), rows, preferred_element_type=jnp.float32).astype(
        jnp.bfloat16
    )
    targets = jnp.sum(placing.astype(jnp.int32) * (slot + 1)[None, :], axis=1) - 1
    return (sent.reshape(shards, capacity, rows.shape[1]), targets.reshape(shards, capacity))


def scatter_items(rows, targets, new_count):
    picking = (jnp.arange(new_count, dtype=jnp.int32)[:, None] == targets[None, :]).astype(
        jnp.bfloat16
    )
    return jnp.dot(picking, rows, preferred_element_type=jnp.float32)


def body(
    hidden, table, new_mask, labels, in_grad, item_owner, item_slot, first_moment, second_moment
):
    blocks = hidden.shape[1]
    width = hidden.shape[3]
    new_count = first_moment.shape[0]
    shards = lax.axis_size("vocab")
    items_here = in_grad.shape[2]
    capacity = max(2, (2 * items_here + shards - 1) // shards)
    vocab_start = lax.axis_index("vocab") * table.shape[0]
    select = select_rows(new_mask, new_count)
    params = jnp.dot(select, table, preferred_element_type=jnp.float32)
    received_rows = []
    received_targets = []
    losses = []
    dstates = []
    full_table = lax.all_gather(table, "dp", axis=1, tiled=True)
    grads = jnp.zeros((new_count, width), jnp.float32)
    for c in range(blocks):
        states = hidden[0, c]
        raw = lax.dot_general(
            states, full_table, (((1,), (1,)), ((), ())), preferred_element_type=jnp.float32
        )
        loss, error = softmax_error(raw, labels[0, c], vocab_start)
        partial_value = jnp.dot(error, full_table, preferred_element_type=jnp.float32)
        dstates.append(finish_hidden(partial_value))
        chosen = lax.dot_general(
            error, select, (((1,), (1,)), ((), ())), preferred_element_type=jnp.float32
        ).astype(jnp.bfloat16)
        grads = grads + lax.dot_general(
            chosen, states, (((0,), (0,)), ((), ())), preferred_element_type=jnp.float32
        )
        losses.append(loss)
        sent_rows, sent_targets = pack_items(
            in_grad[0, c], item_owner[0, c, :, 0], item_slot[0, c], shards, capacity
        )
        got_rows, got_targets = (
            lax.all_to_all(sent_rows, "vocab", split_axis=0, concat_axis=0, tiled=True),
            lax.all_to_all(sent_targets, "vocab", split_axis=0, concat_axis=0, tiled=True),
        )
        received_rows.append(got_rows.reshape(-1, width))
        received_targets.append(got_targets.reshape(-1))
    item_rows = jnp.concatenate(received_rows, axis=0)
    item_targets = jnp.concatenate(received_targets, axis=0)
    grads = grads + scatter_items(item_rows, item_targets, new_count)
    grads = lax.psum_scatter(grads, "dp", scatter_dimension=1, tiled=True)
    first_out = beta_one * first_moment + (1.0 - beta_one) * grads
    second_out = beta_two * second_moment + (1.0 - beta_two) * grads * grads
    update = (
        first_out
        / (1.0 - beta_one**step_count)
        / (jnp.sqrt(second_out / (1.0 - beta_two**step_count)) + epsilon)
        + decay_rate * params
    )
    token_loss = jnp.stack(losses)[None]
    d_hidden = jnp.stack(dstates)[None]
    return (token_loss, d_hidden, update, first_out, second_out)


def solution(mesh):
    return jax.shard_map(
        body,
        mesh=mesh,
        in_specs=(
            P("dp", None, None, None),
            P("vocab", "dp"),
            P("vocab"),
            P("dp", None, None),
            P("dp", None, "vocab", None),
            P("dp", None, "vocab", None),
            P("dp", None, "vocab"),
            P("vocab", "dp"),
            P("vocab", "dp"),
        ),
        out_specs=(
            P("dp", None, None),
            P("dp", None, None, "vocab"),
            P("vocab", "dp"),
            P("vocab", "dp"),
            P("vocab", "dp"),
        ),
        check_vma=False,
    )
```

profile of v0, /device:TPU:1, one launch (start us, length us, event | category | flops | bytes accessed | tf_op | source)
XLA Modules:
  0.0 393.1 jit_solution(2182474801881133417)
XLA Ops:
  9.2 8.6 %all-to-all-start.5 = ((s32[32,1,2]{2,1,0:T(1,128)}), s32[32,1,2]{2,1,0:T(1,128)S(1)}, u32[]{:S(2)}, u32[]{:S(2)}) async-start(s32[32,1,2]{2,1,0:T(1,128)} %bitcast.21), calls=%async_computation.5 | async-start | bytes 32768 | tf_op jit(solution)/shard_map/all_to_all | solution.py:130
  20.2 4.6 %all-to-all-done.5 = s32[32,1,2]{2,1,0:T(1,128)S(1)} async-done(((s32[32,1,2]{2,1,0:T(1,128)}), s32[32,1,2]{2,1,0:T(1,128)S(1)}, u32[]{:S(2)}, u32[]{:S(2)}) %all-to-all-start.5) | async-done | bytes 288 | tf_op jit(solution)/shard_map/all_to_all | solution.py:130
  24.7 4.1 %all-to-all-start.4 = ((s32[32,1,2]{2,1,0:T(1,128)}), s32[32,1,2]{2,1,0:T(1,128)S(1)}, u32[]{:S(2)}, u32[]{:S(2)}) async-start(s32[32,1,2]{2,1,0:T(1,128)} %bitcast.18), calls=%async_computation.4 | async-start | bytes 32768 | tf_op jit(solution)/shard_map/all_to_all | solution.py:130
  28.9 1.0 reshape.176
  32.3 3.6 all-to-all-done.4
  35.9 4.2 %all-to-all-start.7 = ((bf16[32,2,4608]{2,1,0:T(2,128)(2,1)}), bf16[32,2,4608]{2,1,0:T(2,128)(2,1)S(1)}, u32[]{:S(2)}, u32[]{:S(2)}) async-start(bf16[32,2,4608]{2,1,0:T(2,128)(2,1)} %reshape.176), calls=%async_computation.7 | async-start | bytes 1179648 | tf_op jit(solution)/shard_map/all_to_all | solution.py:129
  40.9 187.1 %all-gather.2.cloned.1.call-done = bf16[2304,4608]{0,1:T(8,128)(2,1)} async-done(((bf16[2304,576]{0,1:T(8,128)(2,1)}), bf16[2304,4608]{0,1:T(8,128)(2,1)}) %all-gather.2.cloned.1.call-update) | async-done | bytes 21233680 | tf_op jit(solution)/shard_map/all_gather | solution.py:108
  228.0 9.1 %fusion.1 = f32[64,2304]{1,0:T(8,128)S(1)} fusion(bf16[2304,4608]{0,1:T(8,128)(2,1)} %all-gather.2.cloned.1.call-done, bf16[1,2,64,4608]{3,2,1,0:T(8,128)(2,1)S(1)} %copy-done), kind=kOutput, calls=%fused_computation.7 | convolution fusion | flops 1359101952 | bytes 22413312 | tf_op jit(solution)/shard_map/dot_general | solution.py:112
  237.1 7.8 %all-to-all-start.6 = ((bf16[32,2,4608]{2,1,0:T(2,128)(2,1)}), bf16[32,2,4608]{2,1,0:T(2,128)(2,1)}, u32[]{:S(2)}, u32[]{:S(2)}) async-start(bf16[32,2,4608]{2,1,0:T(2,128)(2,1)} %reshape.174), calls=%async_computation.6 | async-start | bytes 1179648 | tf_op jit(solution)/shard_map/all_to_all | solution.py:129
  244.9 9.2 %exponential_reduce_fusion.1 = (f32[64]{0:T(128)S(1)}, f32[64]{0:T(128)S(1)}, f32[64]{0:T(128)S(1)}, f32[64]{0:T(128)S(1)}, f32[64,2304]{1,0:T(8,128)S(1)}) fusion(s32[64]{0:T(128)S(1)} %get-tuple-element.19, s32[2304]{0:T(1024)S(1)} %iota_add_fusion, s32[64]{0:T(128)S(1)} %get-tuple-element.20, f32[64,2304]{1,0:T(8,128)S(1)} %fusion.1, ...), kind=kOutput, calls=%fused_computation.49 | convolution fusion | flops 1360576512 | bytes 23017472 | tf_op jit(solution)/shard_map/dot_general | solution.py:112
  254.2 3.0 all-to-all-done.6
  257.8 4.4 %all-to-all-start.1 = ((f32[32,1,128]{2,1,0:T(1,128)}), f32[32,1,128]{2,1,0:T(1,128)S(1)}, u32[]{:S(2)}, u32[]{:S(2)}) async-start(f32[32,1,128]{2,1,0:T(1,128)} %broadcast_in_dim.15), calls=%async_computation.1 | async-start | bytes 32768 | tf_op jit(solution)/shard_map/all_to_all | solution.py:16
  262.3 6.8 %all-to-all-done.1 = f32[32,1,128]{2,1,0:T(1,128)S(1)} async-done(((f32[32,1,128]{2,1,0:T(1,128)}), f32[32,1,128]{2,1,0:T(1,128)S(1)}, u32[]{:S(2)}, u32[]{:S(2)}) %all-to-all-start.1) | async-done | bytes 16416 | tf_op jit(solution)/shard_map/all_to_all | solution.py:16
  269.7 4.1 %all-to-all-start = ((f32[32,1,128]{2,1,0:T(1,128)}), f32[32,1,128]{2,1,0:T(1,128)S(1)}, u32[]{:S(2)}, u32[]{:S(2)}) async-start(f32[32,1,128]{2,1,0:T(1,128)} %broadcast_in_dim.14), calls=%async_computation | async-start | bytes 32768 | tf_op jit(solution)/shard_map/all_to_all | solution.py:16
  275.2 2.1 reshape.175
  277.3 3.5 all-to-all-done
  281.0 4.1 %fusion.33 = f32[256,4608]{0,1:T(8,128)} fusion(s32[2304]{0:T(1024)S(1)} %add_bitcast_fusion, pred[2304]{0:T(1024)(128)(4,1)S(1)} %broadcast_compare_fusion, bf16[1,2,64,4608]{3,2,1,0:T(8,128)(2,1)S(1)} %copy-done, f32[64,2304]{1,0:T(8,128)S(1)} %get-tuple-element.25, f32[64]{0:T(128)S(1)} %get-tuple-element.21, s32[2304]{0:T(1024)S(1)} %iota_add_fusion, ...), kind=kOutput, calls=%fused_computation.28 | convolution fusion | flops 229015552 | bytes 5926912 | tf_op jit(solution)/shard_map/dot_general | solution.py:121
  285.0 6.5 %convolution_add_fusion.1 = f32[256,4608]{0,1:T(8,128)} fusion(f32[256,4608]{0,1:T(8,128)} %fusion.33, s32[2304]{0:T(1024)S(1)} %add_bitcast_fusion, pred[2304]{0:T(1024)(128)(4,1)S(1)} %broadcast_compare_fusion, bf16[1,2,64,4608]{3,2,1,0:T(8,128)(2,1)S(1)} %copy-done, f32[64,2304]{1,0:T(8,128)S(1)} %fusion.1, f32[64]{0:T(128)S(1)} %get-tuple-element.27, ...), kind=kOutput, calls=%fused_computation.1 | convolution fusion | flops 230195200 | bytes 10645504 | tf_op jit(solution)/shard_map/dot_general | solution.py:121
  291.5 5.5 %convolution_add_fusion = f32[256,4608]{0,1:T(8,128)} fusion(f32[256,4608]{0,1:T(8,128)} %convolution_add_fusion.1, bf16[64,4608]{1,0:T(8,128)(2,1)S(1)} %copy-done.2, bf16[64,4608]{1,0:T(8,128)(2,1)} %reshape.175, s32[128]{0:T(128)S(1)} %pad_add_fusion), kind=kOutput, calls=%fused_computation | convolution fusion | flops 305561600 | bytes 10617344 | tf_op jit(solution)/shard_map/dot_general | solution.py:89
  297.1 11.7 %fusion.64 = f32[64,4608]{1,0:T(8,128)} fusion(bf16[2304,4608]{0,1:T(8,128)(2,1)} %all-gather.2.cloned.1.call-done, f32[64,2304]{1,0:T(8,128)S(1)} %fusion.1, f32[64]{0:T(128)S(1)} %get-tuple-element.27, s32[2304]{0:T(1024)S(1)} %iota_add_fusion, s32[64]{0:T(128)S(1)} %get-tuple-element.20), kind=kOutput, calls=%fused_computation.96 | convolution fusion | flops 1360281600 | bytes 23012864 | tf_op jit(solution)/shard_map/dot_general | solution.py:116
  308.8 2.7 reshape.169
  311.6 2.5 copy.30
  314.1 4.3 %all-to-all-start.3 = ((f32[32,64,144]{2,1,0:T(8,128)}), f32[32,64,144]{2,1,0:T(8,128)S(1)}, u32[]{:S(2)}, u32[]{:S(2)}) async-start(f32[32,64,144]{2,1,0:T(8,128)} %bitcast.67), calls=%async_computation.3 | async-start | bytes 4194304 | tf_op jit(solution)/shard_map/all_to_all | solution.py:42
  318.4 11.9 %fusion.68 = f32[64,4608]{1,0:T(8,128)} fusion(bf16[2304,4608]{0,1:T(8,128)(2,1)} %all-gather.2.cloned.1.call-done, f32[64,2304]{1,0:T(8,128)S(1)} %get-tuple-element.25, f32[64]{0:T(128)S(1)} %get-tuple-element.21, s32[2304]{0:T(1024)S(1)} %iota_add_fusion, s32[64]{0:T(128)S(1)} %get-tuple-element.19), kind=kOutput, calls=%fused_computation.97 | convolution fusion | flops 1360281600 | bytes 23012864 | tf_op jit(solution)/shard_map/dot_general | solution.py:116
  330.3 3.6 reshape.168
  333.9 4.2 %copy.31 = f32[64,32,144]{2,0,1:T(8,128)} copy(f32[64,32,144]{2,1,0:T(8,128)} %reshape.168) | data formatting | bytes 2359296 | tf_op jit(solution)/shard_map/reshape | solution.py:36
  338.1 8.7 %all-to-all-done.3 = f32[32,64,144]{2,1,0:T(8,128)S(1)} async-done(((f32[32,64,144]{2,1,0:T(8,128)}), f32[32,64,144]{2,1,0:T(8,128)S(1)}, u32[]{:S(2)}, u32[]{:S(2)}) %all-to-all-start.3) | async-done | bytes 1179680 | tf_op jit(solution)/shard_map/all_to_all | solution.py:42
  346.9 5.2 %all-to-all-start.2 = ((f32[32,64,144]{2,1,0:T(8,128)}), f32[32,64,144]{2,1,0:T(8,128)}, u32[]{:S(2)}, u32[]{:S(2)}) async-start(f32[32,64,144]{2,1,0:T(8,128)} %bitcast.66), calls=%async_computation.2 | async-start | bytes 4194304 | tf_op jit(solution)/shard_map/all_to_all | solution.py:42
  352.8 27.7 %all-to-all-done.2 = f32[32,64,144]{2,1,0:T(8,128)} async-done(((f32[32,64,144]{2,1,0:T(8,128)}), f32[32,64,144]{2,1,0:T(8,128)}, u32[]{:S(2)}, u32[]{:S(2)}) %all-to-all-start.2) | async-done | bytes 1179680 | tf_op jit(solution)/shard_map/all_to_all | solution.py:42
  380.5 1.7 reduce_sum.114
  382.9 1.4 multiply_add_fusion
  384.4 1.9 fusion.12
  (70 shorter events, 11.6 us)
Async XLA Ops:
  7.2 0.8 copy-start.8
  7.2 1.2 copy-start.9
  7.2 10.6 %copy-start.7 = (s32[2304]{0:T(1024)S(1)}, s32[2304]{0:T(1024)}, u32[]{:S(2)}) copy-start(s32[2304]{0:T(1024)} %param.11) | copy-start | bytes 27652
  7.2 11.3 %copy-start.10 = (s32[1,2,64]{2,1,0:T(2,128)S(1)}, s32[1,2,64]{2,1,0:T(2,128)}, u32[]{:S(2)}) copy-start(s32[1,2,64]{2,1,0:T(2,128)} %param.12) | copy-start | bytes 1540
  7.2 11.4 %copy-start.6 = (bf16[1,2,24,4608]{3,2,1,0:T(8,128)(2,1)S(1)}, bf16[1,2,24,4608]{3,2,1,0:T(8,128)(2,1)}, u32[]{:S(2)}) copy-start(bf16[1,2,24,4608]{3,2,1,0:T(8,128)(2,1)} %param.13) | copy-start | bytes 1327108
  7.2 220.8 %all-gather.2.cloned.1.call-start = ((), (), s32[]{:S(2)}) async-start(), calls=%async_computation.9 | async-start | bytes 23887872 | tf_op jit(solution)/shard_map/all_gather | solution.py:108
  9.2 15.5 %all-to-all-start.5 = ((s32[32,1,2]{2,1,0:T(1,128)}), s32[32,1,2]{2,1,0:T(1,128)S(1)}, u32[]{:S(2)}, u32[]{:S(2)}) async-start(s32[32,1,2]{2,1,0:T(1,128)} %bitcast.21), calls=%async_computation.5 | async-start | bytes 32768 | tf_op jit(solution)/shard_map/all_to_all | solution.py:130
  19.0 209.0 %copy-start = (bf16[1,2,64,4608]{3,2,1,0:T(8,128)(2,1)S(1)}, bf16[1,2,64,4608]{3,2,1,0:T(8,128)(2,1)}, u32[]{:S(2)}) copy-start(bf16[1,2,64,4608]{3,2,1,0:T(8,128)(2,1)} %param.9) | copy-start | bytes 3538948
  24.7 11.2 %all-to-all-start.4 = ((s32[32,1,2]{2,1,0:T(1,128)}), s32[32,1,2]{2,1,0:T(1,128)S(1)}, u32[]{:S(2)}, u32[]{:S(2)}) async-start(s32[32,1,2]{2,1,0:T(1,128)} %bitcast.18), calls=%async_computation.4 | async-start | bytes 32768 | tf_op jit(solution)/shard_map/all_to_all | solution.py:130
  35.9 201.2 %all-to-all-start.7 = ((bf16[32,2,4608]{2,1,0:T(2,128)(2,1)}), bf16[32,2,4608]{2,1,0:T(2,128)(2,1)S(1)}, u32[]{:S(2)}, u32[]{:S(2)}) async-start(bf16[32,2,4608]{2,1,0:T(2,128)(2,1)} %reshape.176), calls=%async_computation.7 | async-start | bytes 1179648 | tf_op jit(solution)/shard_map/all_to_all | solution.py:129
  237.1 20.1 %all-to-all-start.6 = ((bf16[32,2,4608]{2,1,0:T(2,128)(2,1)}), bf16[32,2,4608]{2,1,0:T(2,128)(2,1)}, u32[]{:S(2)}, u32[]{:S(2)}) async-start(bf16[32,2,4608]{2,1,0:T(2,128)(2,1)} %reshape.174), calls=%async_computation.6 | async-start | bytes 1179648 | tf_op jit(solution)/shard_map/all_to_all | solution.py:129
  257.8 11.3 %all-to-all-start.1 = ((f32[32,1,128]{2,1,0:T(1,128)}), f32[32,1,128]{2,1,0:T(1,128)S(1)}, u32[]{:S(2)}, u32[]{:S(2)}) async-start(f32[32,1,128]{2,1,0:T(1,128)} %broadcast_in_dim.15), calls=%async_computation.1 | async-start | bytes 32768 | tf_op jit(solution)/shard_map/all_to_all | solution.py:16
  269.7 11.2 %all-to-all-start = ((f32[32,1,128]{2,1,0:T(1,128)}), f32[32,1,128]{2,1,0:T(1,128)S(1)}, u32[]{:S(2)}, u32[]{:S(2)}) async-start(f32[32,1,128]{2,1,0:T(1,128)} %broadcast_in_dim.14), calls=%async_computation | async-start | bytes 32768 | tf_op jit(solution)/shard_map/all_to_all | solution.py:16
  273.8 109.1 %reduce-scatter.2.cloned.1.call-start = ((), (), s32[]{:S(2)}) async-start(), calls=%async_computation.10 | async-start | bytes 5308416 | tf_op jit(solution)/shard_map/reduce_scatter | solution.py:137
  285.0 6.5 %copy-start.2 = (bf16[64,4608]{1,0:T(8,128)(2,1)S(1)}, bf16[64,4608]{1,0:T(8,128)(2,1)}, u32[]{:S(2)}) copy-start(bf16[64,4608]{1,0:T(8,128)(2,1)} %reshape.177) | copy-start | bytes 1769476
  314.1 32.8 %all-to-all-start.3 = ((f32[32,64,144]{2,1,0:T(8,128)}), f32[32,64,144]{2,1,0:T(8,128)S(1)}, u32[]{:S(2)}, u32[]{:S(2)}) async-start(f32[32,64,144]{2,1,0:T(8,128)} %bitcast.67), calls=%async_computation.3 | async-start | bytes 4194304 | tf_op jit(solution)/shard_map/all_to_all | solution.py:42
  346.9 33.6 %all-to-all-start.2 = ((f32[32,64,144]{2,1,0:T(8,128)}), f32[32,64,144]{2,1,0:T(8,128)}, u32[]{:S(2)}, u32[]{:S(2)}) async-start(f32[32,64,144]{2,1,0:T(8,128)} %bitcast.66), calls=%async_computation.2 | async-start | bytes 4194304 | tf_op jit(solution)/shard_map/all_to_all | solution.py:42
  352.0 30.9 %copy-start.3 = (f32[256,576]{0,1:T(8,128)S(1)}, f32[256,576]{0,1:T(8,128)}, u32[]{:S(2)}) copy-start(f32[256,576]{0,1:T(8,128)} %param.16) | copy-start | bytes 1769476
  352.8 31.6 %copy-start.1 = (bf16[2304,576]{0,1:T(8,128)(2,1)S(1)}, bf16[2304,576]{0,1:T(8,128)(2,1)}, u32[]{:S(2)}) copy-start(bf16[2304,576]{0,1:T(8,128)(2,1)} %param.10) | copy-start | bytes 7962628
  384.3 1.9 copy-start.4
  384.3 1.9 copy-start.5
Sparse Core Ops, SparseCore 0:
  9.8 218.1 all-gather.1
  297.2 55.2 reduce-scatter.1
where the time goes:
time: 394 us; the launch traced here: 393 us
  waiting for transfers between devices  246 us (62%)
  matrix products  60.8 us (15%)
  starting transfers between devices  43 us (11%)
  local copies, waits for them, and re-layouts  21.9 us (6%)
  between operations  14.4 us (4%)
  other arithmetic  7.26 us (2%)
    all_gather x1, waiting for transfers between devices, body(): full_table = lax.all_gather(table, 'dp', axis=1, tiled=True)  187 us
    all_to_all x2, waiting for transfers between devices, sent_and_summed(): lax.all_to_all(parts, axis, split_axis=0, concat_axis=0, tiled=True)  36.5 us
    dot_general x2, matrix products, body(): jnp.dot(error, full_table, preferred_element_type=jnp.float32)  23.6 us
    dot_general x2, matrix products, body(): lax.dot_general(states, full_table, (((1,), (1,)), ((), ())), preferred_e...  18.3 us
    reshape x4, local copies, waits for them, and re-layouts, in_blocks(): array.reshape(*shape[:dim], peers, shape[dim] // peers, *shape[dim + 1:])  13.1 us
    all_to_all x2, starting transfers between devices, body(): lax.all_to_all(sent_targets, 'vocab', split_axis=0, concat_axis=0, tiled=...  12.7 us
    all_to_all x2, starting transfers between devices, body(): lax.all_to_all(sent_rows, 'vocab', split_axis=0, concat_axis=0, tiled=True)  12 us
    dot_general x2, matrix products, body(): lax.dot_general(chosen, states, (((0,), (0,)), ((), ())), preferred_eleme...  10.6 us
  transfers between devices with their start and end apart: 10, of which 8 were waited for; matrix products, arithmetic and copies ran while one was open for 18% of the time, Pallas kernels for 0%

commit v1 on v0

--- a/solution.py
+++ b/solution.py
@@ -105,7 +105,8 @@
     received_targets = []
     losses = []
     dstates = []
-    full_table = lax.all_gather(table, "dp", axis=1, tiled=True)
+    copies = jnp.concatenate([table] * lax.axis_size("dp"), axis=1)
+    full_table = lax.all_to_all(copies, "dp", 1, 1, tiled=True)
     grads = jnp.zeros((new_count, width), jnp.float32)
     for c in range(blocks):
         states = hidden[0, c]

time: 394 us -> 691 us (1.75)
  waiting for transfers between devices: 246 us -> 515 us
  starting transfers between devices: 43 us -> 55.2 us
  matrix products: 60.8 us -> 70 us
    all_to_all x0 -> x1, waiting for transfers between devices: none -> 456 us  [body(): full_table = lax.all_to_all(copies, 'dp', 1, 1, tiled=True)]
    all_gather x1 -> x0, waiting for transfers between devices: 187 us -> none  [body(): full_table = lax.all_gather(table, 'dp', axis=1, tiled=True)]
    unnamed x22 -> x19, local copies, waits for them, and re-layouts: 0.05 us -> 13.5 us
    reshape x4 -> x0, local copies, waits for them, and re-layouts: 13.1 us -> none  [in_blocks(): array.reshape(*shape[:dim], peers, shape[dim] // peers, *shape[dim + 1:])]
    all_to_all x0 -> x1, starting transfers between devices: none -> 8.32 us  [body(): full_table = lax.all_to_all(copies, 'dp', 1, 1, tiled=True)]
  transfers between devices with their start and end apart: 10 -> 10, of which waited for: 8 -> 7; matrix products, arithmetic and copies ran while one was open for 18% -> 12% of each run, Pallas kernels for 0% -> 0%
where the time goes in v1:
time: 691 us; the launch traced here: 690 us
  waiting for transfers between devices  515 us (75%)
  matrix products  70 us (10%)
  starting transfers between devices  55.2 us (8%)
  local copies, waits for them, and re-layouts  25.9 us (4%)
  between operations  14.2 us (2%)
  other arithmetic  10.3 us (1%)
    all_to_all x1, waiting for transfers between devices, body(): full_table = lax.all_to_all(copies, 'dp', 1, 1, tiled=True)  456 us
    all_to_all x2, waiting for transfers between devices, sent_and_summed(): lax.all_to_all(parts, axis, split_axis=0, concat_axis=0, tiled=True)  40.8 us
    dot_general x2, matrix products, body(): jnp.dot(error, full_table, preferred_element_type=jnp.float32)  26.5 us
    dot_general x2, matrix products, body(): lax.dot_general(states, full_table, (((1,), (1,)), ((), ())), preferred_e...  21.3 us
    all_to_all x2, starting transfers between devices, body(): lax.all_to_all(sent_targets, 'vocab', split_axis=0, concat_axis=0, tiled=...  16 us
  transfers between devices with their start and end apart: 10, of which 7 were waited for; matrix products, arithmetic and copies ran while one was open for 12% of the time, Pallas kernels for 0%

profile of v1, /device:TPU:1, one launch (start us, length us, event | category | flops | bytes accessed | tf_op | source)
XLA Modules:
  0.0 690.2 jit_solution(4353950227982446252)
XLA Ops:
  10.7 8.6 %all-to-all-start.5 = ((s32[32,1,2]{2,1,0:T(1,128)}), s32[32,1,2]{2,1,0:T(1,128)S(1)}, u32[]{:S(2)}, u32[]{:S(2)}) async-start(s32[32,1,2]{2,1,0:T(1,128)} %bitcast.30), calls=%async_computation.5 | async-start | bytes 32768 | tf_op jit(solution)/shard_map/all_to_all | solution.py:131
  19.3 3.4 constant_dynamic-update-slice_fusion.7
  22.7 1.7 constant_dynamic-update-slice_fusion.6
  26.1 1.7 constant_dynamic-update-slice_fusion.4
  33.6 7.4 %all-to-all-start.6 = ((s32[32,1,2]{2,1,0:T(1,128)}), s32[32,1,2]{2,1,0:T(1,128)S(1)}, u32[]{:S(2)}, u32[]{:S(2)}) async-start(s32[32,1,2]{2,1,0:T(1,128)} %bitcast.33), calls=%async_computation.6 | async-start | bytes 32768 | tf_op jit(solution)/shard_map/all_to_all | solution.py:131
  41.0 1.7 constant_dynamic-update-slice_fusion
  42.7 5.2 all-to-all-done.6
  47.9 8.3 %all-to-all-start = ((bf16[2304,8,576]{0,2,1:T(8,128)(2,1)}), bf16[2304,8,576]{0,2,1:T(8,128)(2,1)}, u32[]{:S(2)}, u32[]{:S(2)}) async-start(bf16[2304,8,576]{0,2,1:T(8,128)(2,1)} %bitcast), calls=%async_computation | async-start | bytes 42467328 | tf_op jit(solution)/shard_map/all_to_all | solution.py:109
  63.7 455.9 %all-to-all-done = bf16[2304,8,576]{0,2,1:T(8,128)(2,1)} async-done(((bf16[2304,8,576]{0,2,1:T(8,128)(2,1)}), bf16[2304,8,576]{0,2,1:T(8,128)(2,1)}, u32[]{:S(2)}, u32[]{:S(2)}) %all-to-all-start) | async-done | bytes 21233696 | tf_op jit(solution)/shard_map/all_to_all | solution.py:109
  519.6 4.7 all-to-all-start.7
  524.3 9.2 %fusion.1 = f32[2304,64]{0,1:T(8,128)S(1)} fusion(bf16[2304,4608]{0,1:T(8,128)(2,1)} %bitcast.1, bf16[1,2,64,4608]{3,2,1,0:T(8,128)(2,1)} %param.9), kind=kOutput, calls=%fused_computation.7 | convolution fusion | flops 1359101952 | bytes 22413312 | tf_op jit(solution)/shard_map/dot_general | solution.py:113
  533.5 3.2 all-to-all-done.7
  536.7 4.4 all-to-all-start.8
  541.1 12.1 %fusion.48 = (f32[64]{0:T(128)S(1)}, f32[64]{0:T(128)S(1)}, f32[64]{0:T(128)S(1)}, f32[64]{0:T(128)S(1)}, f32[2304,64]{0,1:T(8,128)}) fusion(s32[64]{0:T(128)S(1)} %get-tuple-element.19, s32[2304]{0:T(1024)S(1)} %iota_add_fusion, s32[64]{0:T(128)S(1)} %get-tuple-element.20, f32[2304,64]{0,1:T(8,128)S(1)} %fusion.1, bf16[2304,4608]{0,1:T(8,128)(2,1)} %bitcast.1, ...), kind=kOutput, calls=%fused_computation.50 | convolution fusion | flops 1360576512 | bytes 23013888 | tf_op jit(solution)/shard_map/dot_general | solution.py:113
  554.0 7.3 %all-to-all-start.2 = ((f32[32,1,128]{2,1,0:T(1,128)}), f32[32,1,128]{2,1,0:T(1,128)S(1)}, u32[]{:S(2)}, u32[]{:S(2)}) async-start(f32[32,1,128]{2,1,0:T(1,128)} %broadcast_in_dim.15), calls=%async_computation.2 | async-start | bytes 32768 | tf_op jit(solution)/shard_map/all_to_all | solution.py:16
  561.4 6.8 all-to-all-done.2
  568.8 4.1 all-to-all-start.1
  573.2 2.1 reshape.173
  575.3 2.1 reshape.175
  577.5 2.5 all-to-all-done.1
  580.0 5.3 fusion.33
  585.4 6.6 convolution_add_fusion.1
  592.0 5.7 convolution_add_fusion
  597.7 12.8 %convolution_bitcast_fusion.1 = f32[32,64,144]{2,1,0:T(8,128)} fusion(bf16[32,144,2304]{2,1,0:T(8,128)(2,1)} %bitcast.16, f32[2304,64]{0,1:T(8,128)} %get-tuple-element.25, f32[64]{0:T(128)S(1)} %get-tuple-element.21, s32[2304]{0:T(1024)S(1)} %iota_add_fusion, s32[64]{0:T(128)S(1)} %get-tuple-element.19), kind=kOutput, calls=%fused_computation.14 | convolution fusion | flops 1360281600 | bytes 23012864 | tf_op jit(solution)/shard_map/dot_general | solution.py:117
  610.5 5.1 all-to-all-start.3
  615.6 13.7 %convolution_bitcast_fusion = f32[32,64,144]{2,1,0:T(8,128)} fusion(bf16[32,144,2304]{2,1,0:T(8,128)(2,1)} %bitcast.16, f32[2304,64]{0,1:T(8,128)S(1)} %fusion.1, f32[64]{0:T(128)S(1)} %get-tuple-element.27, s32[2304]{0:T(1024)S(1)} %iota_add_fusion, s32[64]{0:T(128)S(1)} %get-tuple-element.20), kind=kOutput, calls=%fused_computation.13 | convolution fusion | flops 1360281600 | bytes 23012864 | tf_op jit(solution)/shard_map/dot_general | solution.py:117
  629.3 14.7 %all-to-all-done.3 = f32[32,64,144]{2,1,0:T(8,128)} async-done(((f32[32,64,144]{2,1,0:T(8,128)}), f32[32,64,144]{2,1,0:T(8,128)}, u32[]{:S(2)}, u32[]{:S(2)}) %all-to-all-start.3) | async-done | bytes 1179680 | tf_op jit(solution)/shard_map/all_to_all | solution.py:42
  644.0 5.2 all-to-all-start.4
  649.7 1.8 reduce_sum.114
  651.5 26.1 %all-to-all-done.4 = f32[32,64,144]{2,1,0:T(8,128)} async-done(((f32[32,64,144]{2,1,0:T(8,128)}), f32[32,64,144]{2,1,0:T(8,128)}, u32[]{:S(2)}, u32[]{:S(2)}) %all-to-all-start.4) | async-done | bytes 1179680 | tf_op jit(solution)/shard_map/all_to_all | solution.py:42
  677.6 1.7 reduce_sum.115
  681.5 1.9 fusion.12
  (63 shorter events, 22.9 us)
Async XLA Ops:
  7.2 15.5 %copy-start = (bf16[2304,576]{0,1:T(8,128)(2,1)S(1)}, bf16[2304,576]{0,1:T(8,128)(2,1)}, u32[]{:S(2)}) copy-start(bf16[2304,576]{0,1:T(8,128)(2,1)} %param.10) | copy-start | bytes 7962628
  10.7 22.9 %all-to-all-start.5 = ((s32[32,1,2]{2,1,0:T(1,128)}), s32[32,1,2]{2,1,0:T(1,128)S(1)}, u32[]{:S(2)}, u32[]{:S(2)}) async-start(s32[32,1,2]{2,1,0:T(1,128)} %bitcast.30), calls=%async_computation.5 | async-start | bytes 32768 | tf_op jit(solution)/shard_map/all_to_all | solution.py:131
  33.6 14.3 %all-to-all-start.6 = ((s32[32,1,2]{2,1,0:T(1,128)}), s32[32,1,2]{2,1,0:T(1,128)S(1)}, u32[]{:S(2)}, u32[]{:S(2)}) async-start(s32[32,1,2]{2,1,0:T(1,128)} %bitcast.33), calls=%async_computation.6 | async-start | bytes 32768 | tf_op jit(solution)/shard_map/all_to_all | solution.py:131
  47.8 8.3 %copy-start.4 = (s32[2304]{0:T(1024)S(1)}, s32[2304]{0:T(1024)}, u32[]{:S(2)}) copy-start(s32[2304]{0:T(1024)} %param.11) | copy-start | bytes 27652
  47.9 13.7 %copy-start.5 = (s32[1,2,64]{2,1,0:T(2,128)S(1)}, s32[1,2,64]{2,1,0:T(2,128)}, u32[]{:S(2)}) copy-start(s32[1,2,64]{2,1,0:T(2,128)} %param.12) | copy-start | bytes 1540
  47.9 471.8 %all-to-all-start = ((bf16[2304,8,576]{0,2,1:T(8,128)(2,1)}), bf16[2304,8,576]{0,2,1:T(8,128)(2,1)}, u32[]{:S(2)}, u32[]{:S(2)}) async-start(bf16[2304,8,576]{0,2,1:T(8,128)(2,1)} %bitcast), calls=%async_computation | async-start | bytes 42467328 | tf_op jit(solution)/shard_map/all_to_all | solution.py:109
  519.6 17.1 %all-to-all-start.7 = ((bf16[32,2,4608]{2,1,0:T(2,128)(2,1)}), bf16[32,2,4608]{2,1,0:T(2,128)(2,1)}, u32[]{:S(2)}, u32[]{:S(2)}) async-start(bf16[32,2,4608]{2,1,0:T(2,128)(2,1)} %reshape.172), calls=%async_computation.7 | async-start | bytes 1179648 | tf_op jit(solution)/shard_map/all_to_all | solution.py:130
  536.7 16.6 %all-to-all-start.8 = ((bf16[32,2,4608]{2,1,0:T(2,128)(2,1)}), bf16[32,2,4608]{2,1,0:T(2,128)(2,1)}, u32[]{:S(2)}, u32[]{:S(2)}) async-start(bf16[32,2,4608]{2,1,0:T(2,128)(2,1)} %reshape.174), calls=%async_computation.8 | async-start | bytes 1179648 | tf_op jit(solution)/shard_map/all_to_all | solution.py:130
  554.0 14.2 %all-to-all-start.2 = ((f32[32,1,128]{2,1,0:T(1,128)}), f32[32,1,128]{2,1,0:T(1,128)S(1)}, u32[]{:S(2)}, u32[]{:S(2)}) async-start(f32[32,1,128]{2,1,0:T(1,128)} %broadcast_in_dim.15), calls=%async_computation.2 | async-start | bytes 32768 | tf_op jit(solution)/shard_map/all_to_all | solution.py:16
  568.8 11.2 %all-to-all-start.1 = ((f32[32,1,128]{2,1,0:T(1,128)}), f32[32,1,128]{2,1,0:T(1,128)S(1)}, u32[]{:S(2)}, u32[]{:S(2)}) async-start(f32[32,1,128]{2,1,0:T(1,128)} %broadcast_in_dim.14), calls=%async_computation.1 | async-start | bytes 32768 | tf_op jit(solution)/shard_map/all_to_all | solution.py:16
  572.9 107.1 %reduce-scatter.2.cloned.1.call-start = ((), (), s32[]{:S(2)}) async-start(), calls=%async_computation.10 | async-start | bytes 5308416 | tf_op jit(solution)/shard_map/reduce_scatter | solution.py:138
  610.5 33.5 %all-to-all-start.3 = ((f32[32,64,144]{2,1,0:T(8,128)}), f32[32,64,144]{2,1,0:T(8,128)}, u32[]{:S(2)}, u32[]{:S(2)}) async-start(f32[32,64,144]{2,1,0:T(8,128)} %convolution_bitcast_fusion.1), calls=%async_computation.3 | async-start | bytes 4194304 | tf_op jit(solution)/shard_map/all_to_all | solution.py:42
  629.3 50.7 %copy-start.1 = (f32[256,576]{0,1:T(8,128)S(1)}, f32[256,576]{0,1:T(8,128)}, u32[]{:S(2)}) copy-start(f32[256,576]{0,1:T(8,128)} %param.16) | copy-start | bytes 1769476
  644.0 33.6 %all-to-all-start.4 = ((f32[32,64,144]{2,1,0:T(8,128)}), f32[32,64,144]{2,1,0:T(8,128)}, u32[]{:S(2)}, u32[]{:S(2)}) async-start(f32[32,64,144]{2,1,0:T(8,128)} %convolution_bitcast_fusion), calls=%async_computation.4 | async-start | bytes 4194304 | tf_op jit(solution)/shard_map/all_to_all | solution.py:42
  681.4 1.9 copy-start.2
  681.4 1.9 copy-start.3
Sparse Core Ops, SparseCore 0:
  597.9 54.0 reduce-scatter.1
